TPU v7x, 32 devices: a whole 2x2x4 slice. The times are simulated.
32 devices in a mesh: px: 4 (over y, x), py: 8 (over z, core).
Axes of the slice: x: 2, y: 2, z: 4, core: 2. Of those that a mesh axis runs over, the one named last changes fastest.
Arguments:
- coefficients: bfloat16 [384, 12288], P(('px', 'py')), may hold values from -6 to 6
- exponents: int32 [96, 768], P(('px', 'py')), may hold values from -4 to 1
- right_side: float32 [64, 192, 384], P('px', 'py'), may hold values from -18 to 18
Outputs:
- decoded: float32 [64, 192, 384], P('px', 'py')
- residual: float32 [64, 192, 384], P('px', 'py')
- rms: float32 [], replicated
All inputs are finite; a program needn't handle non-finite values.
Results may differ from a plain program's by a relative error of at most 0.0003.
Values may be sent and summed in bfloat16 or wider, within the bound.
No kernel may reach another device: no remote copies, remote signals or barrier semaphores. Data moves between devices by JAX's collectives and lax.ppermute only.
A program may use at most 64 MiB of HBM per device.

v0:
```python
import jax
import jax.numpy as jnp
from jax import lax
from jax.sharding import PartitionSpec as P

CX = 16
CY = 24


def with_halo(cells, sides, width):
    for axis, dim in sides:
        count = lax.axis_size(axis)
        ends = count - 1
        head = lax.slice_in_dim(cells, 0, width, axis=dim)
        tail = lax.slice_in_dim(cells, cells.shape[dim] - width, cells.shape[dim], axis=dim)
        cells = jnp.concatenate(
            [
                lax.ppermute(tail, axis, [(i, (i + 1) % count) for i in range(ends)]),
                cells,
                lax.ppermute(head, axis, [((i + 1) % count, i) for i in range(ends)]),
            ],
            axis=dim,
        )
    return cells


def block_basis(width):
    rows = jnp.arange(width, dtype=jnp.int32)[:, None]
    cols = jnp.arange(width, dtype=jnp.int32)[None, :]
    frequency = (rows % 4).astype(jnp.float32)
    point = (cols % 4).astype(jnp.float32)
    weight = jnp.where(frequency == 0, jnp.sqrt(jnp.float32(0.25)), jnp.sqrt(jnp.float32(0.5)))
    entry = weight * jnp.cos(jnp.pi * (2.0 * point + 1.0) * frequency / 8.0)
    return jnp.where(rows // 4 == cols // 4, entry, 0.0)


def plane_table():
    across_x = block_basis(CX)
    across_y = block_basis(CY)
    return jnp.einsum("ux,vy->uvxy", across_x, across_y).reshape(CX * CY, CX * CY)


def spread_table():
    quarter_y = CY // 4
    blocks = jnp.arange(CX // 4 * quarter_y, dtype=jnp.int32)[:, None]
    cells = jnp.arange(CX * CY, dtype=jnp.int32)[None, :]
    same_x = cells // CY // 4 == blocks // quarter_y
    same_y = cells % CY // 4 == blocks % quarter_y
    return jnp.where(same_x & same_y, 1.0, 0.0).astype(jnp.float32)


def apply_plane(layers, table):
    return jnp.einsum(
        "zpc,cv->zpv", layers.astype(jnp.float32), table, precision=lax.Precision.HIGHEST
    )


def shards(coefficients, exponents, right_side):
    count_x = lax.axis_size("px")
    count_y = lax.axis_size("py")
    peers = count_x * count_y
    patch = CX * CY
    layer_count = coefficients.shape[0]
    block_layers = exponents.shape[0]
    table = plane_table()
    factor = jnp.exp2(exponents.astype(jnp.float32)).reshape(block_layers, peers, -1)
    spread = jnp.einsum("zpq,qc->zpc", factor, spread_table(), precision=lax.Precision.HIGHEST)
    spread = jnp.broadcast_to(spread[:, None], (block_layers, 4, peers, patch)).reshape(
        layer_count, peers, patch
    )
    scaled = (coefficients.astype(jnp.float32).reshape(layer_count, peers, patch) * spread).astype(
        jnp.bfloat16
    )
    received = lax.all_to_all(scaled, ("px", "py"), split_axis=1, concat_axis=1, tiled=True)
    arrived = apply_plane(received, table)
    stacked = arrived.transpose(1, 0, 2).reshape(-1, 128, patch)
    depth_table = block_basis(128)
    decoded = jnp.einsum(
        "nzq,zw->qnw", stacked, depth_table, precision=lax.Precision.HIGHEST
    ).reshape(CX, CY, -1)
    padded = with_halo(decoded, (("px", 0), ("py", 1)), 1)
    padded = jnp.pad(padded, ((0, 0), (0, 0), (1, 1)))
    beside = padded[2:, 1:-1, 1:-1] + padded[:-2, 1:-1, 1:-1]
    beside = beside + padded[1:-1, 2:, 1:-1] + padded[1:-1, :-2, 1:-1]
    beside = beside + padded[1:-1, 1:-1, 2:] + padded[1:-1, 1:-1, :-2]
    residual = right_side - (6.0 * decoded - beside)
    local_sum = jnp.sum(residual * residual)
    total_sum = lax.psum(local_sum, ("px", "py"))
    cell_count = decoded.shape[0] * decoded.shape[1] * decoded.shape[2] * count_x * count_y
    rms = jnp.sqrt(total_sum / cell_count + 1e-06)
    return (decoded, residual, rms)


def solution(mesh):
    return jax.shard_map(
        shards,
        mesh=mesh,
        in_specs=(P(("px", "py"), None), P(("px", "py"), None), P("px", "py", None)),
        out_specs=(P("px", "py", None), P("px", "py", None), P()),
        check_vma=False,
    )
```

profile of v0, /device:TPU:0, one launch (start us, length us, event | category | flops | bytes accessed | tf_op | source)
XLA Modules:
  0.0 87.5 jit_solution(5199137240304117079)
XLA Ops:
  0.7 0.7 multiply_exponential_fusion
  1.4 0.1 reshape.520
  1.5 1.1 %reshape.525 = f32[12,12288]{1,0:T(8,128)S(1)} convert(bf16[12,12288]{1,0:T(8,128)(2,1)} %param.3) | non-fusion elementwise | flops 147456 | bytes 884736 | tf_op jit(solution)/shard_map/reshape | solution.py:71
  2.5 0.2 copy.34
  2.7 0.3 fusion.15
  3.0 0.1 fusion.1
  3.1 0.8 copy.27
  3.9 7.3 %all-to-all-start = ((bf16[12,32,384]{2,0,1:T(8,128)(2,1)}), bf16[12,32,384]{2,0,1:T(8,128)(2,1)S(1)}, u32[]{:S(2)}, u32[]{:S(2)}) async-start(bf16[12,32,384]{2,0,1:T(8,128)(2,1)} %copy.27), calls=%async_computation | async-start | bytes 786432 | tf_op jit(solution)/shard_map/all_to_all | solution.py:74
  11.3 0.1 multiply_select_fusion
  11.5 0.1 multiply_select_fusion.1
  11.6 0.3 multiply_bitcast_fusion
  11.9 2.3 %reshape.528 = f32[384,384,1]{1,0,2:T(8,128)} reshape(f32[16,24,16,24]{3,2,1,0:T(8,128)S(1)} %multiply_bitcast_fusion) | data formatting | bytes 1179648 | tf_op jit(solution)/shard_map/reshape | solution.py:40
  14.3 10.4 %all-to-all-done = bf16[12,32,384]{2,0,1:T(8,128)(2,1)S(1)} async-done(((bf16[12,32,384]{2,0,1:T(8,128)(2,1)}), bf16[12,32,384]{2,0,1:T(8,128)(2,1)S(1)}, u32[]{:S(2)}, u32[]{:S(2)}) %all-to-all-start) | async-done | bytes 294944 | tf_op jit(solution)/shard_map/all_to_all | solution.py:74
  24.7 1.8 %convolution_bitcast_fusion.1 = f32[32,12,384]{2,0,1:T(8,128)S(1)} fusion(f32[384,384,1]{1,0,2:T(8,128)} %reshape.528, bf16[12,32,384]{2,0,1:T(8,128)(2,1)S(1)} %all-to-all-done), kind=kOutput, calls=%fused_computation.4 | convolution fusion | flops 679477248 | bytes 1474560 | tf_op jit(solution)/shard_map/zpc,cv->zpv/dot_general | solution.py:53
  26.5 0.4 copy.29
  26.9 0.1 reshape.523
  27.0 0.9 %convolution_bitcast_fusion = f32[384,3,128]{0,2,1:T(8,128)S(1)} fusion(f32[3,128,384]{2,1,0:T(8,128)S(1)} %reshape.523, f32[128]{0:T(128)S(1)} %get-tuple-element.27, f32[128]{0:T(128)S(1)} %get-tuple-element.25, f32[128]{0:T(128)S(1)} %get-tuple-element.24, s32[128]{0:T(128)S(1)} %get-tuple-element.26), kind=kOutput, calls=%fused_computation.3 | convolution fusion | flops 226574336 | bytes 1181696 | tf_op jit(solution)/shard_map/nzq,zw->qnw/dot_general | solution.py:78
  27.9 0.1 fusion.54
  28.0 0.1 copy.32
  28.1 1.5 %collective-permute-start.1 = (f32[1,24,384]{2,1,0:T(8,128)S(1)}, f32[1,24,384]{2,1,0:T(8,128)S(1)}, u32[]{:S(2)}, u32[]{:S(2)}) collective-permute-start(f32[1,24,384]{2,1,0:T(8,128)S(1)} %copy.32), channel_id=1, source_target_pairs={{0,8},{8,16},{16,24},{1,9},{9,17},{17,25},{2,10},{10,18},{18,26},{... | collective-permute-start | bytes 110600 | tf_op jit(solution)/shard_map/ppermute | solution.py:18
  29.6 0.3 copy.30
  29.9 0.3 reshape.524
  30.3 0.0 copy-start
  30.3 0.1 copy.31
  30.4 1.3 %collective-permute-start = (f32[1,24,384]{2,1,0:T(8,128)S(1)}, f32[1,24,384]{2,1,0:T(8,128)S(1)}, u32[]{:S(2)}, u32[]{:S(2)}) collective-permute-start(f32[1,24,384]{2,1,0:T(8,128)S(1)} %copy.31), channel_id=1, source_target_pairs={{8,0},{16,8},{24,16},{9,1},{17,9},{25,17},{10,2},{18,10},{26,18},{... | collective-permute-start | bytes 110600 | tf_op jit(solution)/shard_map/ppermute | solution.py:20
  31.7 0.0 collective-permute-done.1
  31.7 0.0 copy-start.1
  31.8 4.9 %collective-permute-done = f32[1,24,384]{2,1,0:T(8,128)S(1)} collective-permute-done((f32[1,24,384]{2,1,0:T(8,128)S(1)}, f32[1,24,384]{2,1,0:T(8,128)S(1)}, u32[]{:S(2)}, u32[]{:S(2)}) %collective-permute-start) | collective-permute-done | bytes 36896 | tf_op jit(solution)/shard_map/ppermute | solution.py:20
  36.8 1.3 %collective-permute-start.2 = (f32[18,1,384]{2,1,0:T(1,128)S(1)}, f32[18,1,384]{2,1,0:T(1,128)S(1)}, u32[]{:S(2)}, u32[]{:S(2)}) collective-permute-start(f32[18,1,384]{2,1,0:T(1,128)S(1)} %get-tuple-element.9), channel_id=1, source_target_pairs={{1,0},{2,1},{3,2},{4,3},{5,4},{6,5},{7,6},{9,8},{10,9},{11,10},{12... | collective-permute-start | bytes 82952 | tf_op jit(solution)/shard_map/ppermute | solution.py:20
  38.1 3.0 %collective-permute-start.3 = (f32[18,1,384]{2,1,0:T(1,128)S(1)}, f32[18,1,384]{2,1,0:T(1,128)S(1)}, u32[]{:S(2)}, u32[]{:S(2)}) collective-permute-start(f32[18,1,384]{2,1,0:T(1,128)S(1)} %get-tuple-element.8), channel_id=1, source_target_pairs={{0,1},{1,2},{2,3},{3,4},{4,5},{5,6},{6,7},{8,9},{9,10},{10,11},{11... | collective-permute-start | bytes 82952 | tf_op jit(solution)/shard_map/ppermute | solution.py:18
  41.1 0.0 collective-permute-done.2
  41.1 0.8 collective-permute-done.3
  41.9 0.6 select_maximum_fusion
  42.5 0.0 copy-done
  42.5 0.0 copy-done.1
  42.5 1.9 %multiply_reduce_fusion = (f32[]{:T(128)}, f32[16,24,384]{2,1,0:T(8,128)}) fusion(f32[16,24,384]{2,1,0:T(8,128)S(1)} %copy-done.1, f32[18,26,386]{2,1,0:T(8,128)S(1)} %select_maximum_fusion, f32[18,24,384]{2,1,0:T(8,128)S(1)} %constant_dynamic-update-slice_fusion, f32[18,1,384]{2,1,0:T(1,128)S(1)} %collective-permute-done.3, ...), kind=kLoop, calls=%fused_computation.21 | loop fusion | flops 2064383 | bytes 3741700 | tf_op jit(solution)/shard_map/reduce_sum | solution.py:87
  44.4 41.2 %psum.7 = f32[]{:T(128)} all-reduce(f32[]{:T(128)} %get-tuple-element.6), channel_id=1, replica_groups=mesh['px'=4,'py'=8] {'px','py'}, use_global_device_ids=true, to_apply=%region_1.2 | all-reduce | flops 1 | bytes 8 | tf_op jit(solution)/shard_map/psum | solution.py:88
  (12 shorter events, 0.2 us)
Async XLA Ops:
  3.9 20.8 %all-to-all-start = ((bf16[12,32,384]{2,0,1:T(8,128)(2,1)}), bf16[12,32,384]{2,0,1:T(8,128)(2,1)S(1)}, u32[]{:S(2)}, u32[]{:S(2)}) async-start(bf16[12,32,384]{2,0,1:T(8,128)(2,1)} %copy.27), calls=%async_computation | async-start | bytes 786432 | tf_op jit(solution)/shard_map/all_to_all | solution.py:74
  28.1 3.6 %collective-permute-start.1 = (f32[1,24,384]{2,1,0:T(8,128)S(1)}, f32[1,24,384]{2,1,0:T(8,128)S(1)}, u32[]{:S(2)}, u32[]{:S(2)}) collective-permute-start(f32[1,24,384]{2,1,0:T(8,128)S(1)} %copy.32), channel_id=1, source_target_pairs={{0,8},{8,16},{16,24},{1,9},{9,17},{17,25},{2,10},{10,18},{18,26},{... | collective-permute-start | bytes 110600 | tf_op jit(solution)/shard_map/ppermute | solution.py:18
  30.3 12.3 %copy-start = (f32[16,24,384]{2,1,0:T(8,128)}, f32[16,24,384]{2,1,0:T(8,128)S(1)}, u32[]{:S(2)}) copy-start(f32[16,24,384]{2,1,0:T(8,128)S(1)} %reshape.524) | copy-start | bytes 1769476
  30.4 6.3 %collective-permute-start = (f32[1,24,384]{2,1,0:T(8,128)S(1)}, f32[1,24,384]{2,1,0:T(8,128)S(1)}, u32[]{:S(2)}, u32[]{:S(2)}) collective-permute-start(f32[1,24,384]{2,1,0:T(8,128)S(1)} %copy.31), channel_id=1, source_target_pairs={{8,0},{16,8},{24,16},{9,1},{17,9},{25,17},{10,2},{18,10},{26,18},{... | collective-permute-start | bytes 110600 | tf_op jit(solution)/shard_map/ppermute | solution.py:20
  31.7 10.8 %copy-start.1 = (f32[16,24,384]{2,1,0:T(8,128)S(1)}, f32[16,24,384]{2,1,0:T(8,128)}, u32[]{:S(2)}) copy-start(f32[16,24,384]{2,1,0:T(8,128)} %param.5) | copy-start | bytes 1769476
  36.8 4.3 %collective-permute-start.2 = (f32[18,1,384]{2,1,0:T(1,128)S(1)}, f32[18,1,384]{2,1,0:T(1,128)S(1)}, u32[]{:S(2)}, u32[]{:S(2)}) collective-permute-start(f32[18,1,384]{2,1,0:T(1,128)S(1)} %get-tuple-element.9), channel_id=1, source_target_pairs={{1,0},{2,1},{3,2},{4,3},{5,4},{6,5},{7,6},{9,8},{10,9},{11,10},{12... | collective-permute-start | bytes 82952 | tf_op jit(solution)/shard_map/ppermute | solution.py:20
  38.1 3.9 %collective-permute-start.3 = (f32[18,1,384]{2,1,0:T(1,128)S(1)}, f32[18,1,384]{2,1,0:T(1,128)S(1)}, u32[]{:S(2)}, u32[]{:S(2)}) collective-permute-start(f32[18,1,384]{2,1,0:T(1,128)S(1)} %get-tuple-element.8), channel_id=1, source_target_pairs={{0,1},{1,2},{2,3},{3,4},{4,5},{5,6},{6,7},{8,9},{9,10},{10,11},{11... | collective-permute-start | bytes 82952 | tf_op jit(solution)/shard_map/ppermute | solution.py:18
where the time goes:
time: 88.1 us; the launch traced here: 87.5 us
  blocking collectives  41.2 us (47%)
  waiting for transfers between devices  16.2 us (18%)
  starting transfers between devices  14.5 us (16%)
  other arithmetic  4.98 us (6%)
  local copies, waits for them, and re-layouts  4.87 us (6%)
  matrix products  3.05 us (3%)
  between operations  2.71 us (3%)
    psum x1, blocking collectives, shards(): total_sum = lax.psum(local_sum, ('px', 'py'))  41.2 us
    all_to_all x1, waiting for transfers between devices, shards(): lax.all_to_all(scaled, ('px', 'py'), split_axis=1, concat_axis=1, tiled=T...  10.4 us
    all_to_all x1, starting transfers between devices, shards(): lax.all_to_all(scaled, ('px', 'py'), split_axis=1, concat_axis=1, tiled=T...  7.33 us
    ppermute x2, waiting for transfers between devices, with_halo(): lax.ppermute(head, axis, [((i + 1) % count, i) for i in range(ends)])  4.95 us
    ppermute x2, starting transfers between devices, with_halo(): lax.ppermute(tail, axis, [(i, (i + 1) % count) for i in range(ends)])  4.57 us
    ppermute x2, starting transfers between devices, with_halo(): lax.ppermute(head, axis, [((i + 1) % count, i) for i in range(ends)])  2.59 us
    reshape x1, local copies, waits for them, and re-layouts, plane_table(): jnp.einsum('ux,vy->uvxy', across_x, across_y).reshape(CX * CY, CX * CY)  2.34 us
    reduce_sum x1, other arithmetic, shards(): local_sum = jnp.sum(residual * residual)  1.91 us
  transfers between devices with their start and end apart: 5, of which 3 were waited for; matrix products, arithmetic and copies ran while one was open for 4% of the time, Pallas kernels for 0%

commit v1 on v0

--- a/solution.py
+++ b/solution.py
@@ -1,10 +1,24 @@
+import functools
 import jax
 import jax.numpy as jnp
 from jax import lax
 from jax.sharding import PartitionSpec as P
+from jax.lax import all_to_all, axis_size
 
 CX = 16
 CY = 24
+
+
+def set_runs(view, peer_axis):
+    current_block = axis_size(peer_axis)
+    outcome_arr = jnp.split(view, current_block, axis=1)
+    v1 = jnp.stack(outcome_arr)
+    spare = all_to_all(v1, axis_name=peer_axis, split_axis=0, concat_axis=0)
+    f_next = jnp.concatenate(spare, axis=1)
+    return f_next
+
+
+point_the_members_all = functools.partial(set_runs, peer_axis=("px", "py"))
 
 
 def with_halo(cells, sides, width):
@@ -71,7 +85,7 @@
     scaled = (coefficients.astype(jnp.float32).reshape(layer_count, peers, patch) * spread).astype(
         jnp.bfloat16
     )
-    received = lax.all_to_all(scaled, ("px", "py"), split_axis=1, concat_axis=1, tiled=True)
+    received = point_the_members_all(scaled)
     arrived = apply_plane(received, table)
     stacked = arrived.transpose(1, 0, 2).reshape(-1, 128, patch)
     depth_table = block_basis(128)

time: 88.1 us -> 106 us (1.20)
  local copies, waits for them, and re-layouts: 4.87 us -> 23.8 us
    unnamed x7 -> x40, local copies, waits for them, and re-layouts: 0.21 us -> 18.9 us
where the time goes in v1:
time: 106 us
  blocking collectives  41.2 us (39%)
  local copies, waits for them, and re-layouts  23.8 us (22%)
  waiting for transfers between devices  16.2 us (15%)
  starting transfers between devices  14.5 us (14%)
  other arithmetic  4.28 us (4%)
  matrix products  3.05 us (3%)
  between operations  2.75 us (3%)
    psum x1, blocking collectives, shards(): total_sum = lax.psum(local_sum, ('px', 'py'))  41.2 us
    unnamed x40, local copies, waits for them, and re-layouts  18.9 us
    all_to_all x1, waiting for transfers between devices, set_runs(): spare = all_to_all(v1, axis_name=peer_axis, split_axis=0, concat_axis=0)  10.4 us
    all_to_all x1, starting transfers between devices, set_runs(): spare = all_to_all(v1, axis_name=peer_axis, split_axis=0, concat_axis=0)  7.33 us
    ppermute x2, waiting for transfers between devices, with_halo(): lax.ppermute(head, axis, [((i + 1) % count, i) for i in range(ends)])  4.95 us
    ppermute x2, starting transfers between devices, with_halo(): lax.ppermute(tail, axis, [(i, (i + 1) % count) for i in range(ends)])  4.57 us
    ppermute x2, starting transfers between devices, with_halo(): lax.ppermute(head, axis, [((i + 1) % count, i) for i in range(ends)])  2.59 us
    reshape x1, local copies, waits for them, and re-layouts, plane_table(): jnp.einsum('ux,vy->uvxy', across_x, across_y).reshape(CX * CY, CX * CY)  2.34 us
  transfers between devices with their start and end apart: 5, of which 3 were waited for; matrix products, arithmetic and copies ran while one was open for 4% of the time, Pallas kernels for 0%

profile of v1, /device:TPU:0, one launch (start us, length us, event | category | flops | bytes accessed | tf_op | source)
XLA Modules:
  0.0 105.8 jit_solution(1550527190100074979)
XLA Ops:
  0.7 0.0 copy-start.2
  0.7 1.1 reshape.533
  1.7 0.2 copy.1225
  1.9 0.1 reshape.526
  2.0 0.3 fusion.16
  2.4 0.1 fusion.1
  2.4 0.2 fusion.57
  2.6 0.3 fusion.56
  2.9 0.6 constant_dynamic-update-slice_fusion.31
  3.5 0.6 constant_dynamic-update-slice_fusion.30
  4.1 0.6 constant_dynamic-update-slice_fusion.29
  4.7 0.6 constant_dynamic-update-slice_fusion.28
  5.3 0.6 constant_dynamic-update-slice_fusion.27
  5.9 0.6 constant_dynamic-update-slice_fusion.26
  6.5 0.6 constant_dynamic-update-slice_fusion.25
  7.1 0.6 constant_dynamic-update-slice_fusion.24
  7.7 0.6 constant_dynamic-update-slice_fusion.23
  8.4 0.6 constant_dynamic-update-slice_fusion.22
  9.0 0.6 constant_dynamic-update-slice_fusion.21
  9.6 0.6 constant_dynamic-update-slice_fusion.20
  10.2 0.6 constant_dynamic-update-slice_fusion.19
  10.8 0.6 constant_dynamic-update-slice_fusion.18
  11.4 0.6 constant_dynamic-update-slice_fusion.17
  12.0 0.6 constant_dynamic-update-slice_fusion.16
  12.6 0.6 constant_dynamic-update-slice_fusion.15
  13.2 0.6 constant_dynamic-update-slice_fusion.14
  13.8 0.6 constant_dynamic-update-slice_fusion.13
  14.4 0.6 constant_dynamic-update-slice_fusion.12
  15.0 0.6 constant_dynamic-update-slice_fusion.11
  15.6 0.6 constant_dynamic-update-slice_fusion.10
  16.2 0.6 constant_dynamic-update-slice_fusion.9
  16.8 0.6 constant_dynamic-update-slice_fusion.8
  17.4 0.6 constant_dynamic-update-slice_fusion.7
  18.0 0.6 constant_dynamic-update-slice_fusion.6
  18.6 0.6 constant_dynamic-update-slice_fusion.5
  19.2 0.6 constant_dynamic-update-slice_fusion.4
  19.8 0.6 constant_dynamic-update-slice_fusion.3
  20.4 0.6 constant_dynamic-update-slice_fusion.2
  21.0 0.6 constant_dynamic-update-slice_fusion.1
  21.6 0.6 constant_dynamic-update-slice_fusion
  22.2 7.3 %all-to-all-start = ((bf16[32,12,1,384]{3,1,2,0:T(8,128)(2,1)}), bf16[32,12,1,384]{3,1,2,0:T(8,128)(2,1)S(1)}, u32[]{:S(2)}, u32[]{:S(2)}) async-start(bf16[32,12,1,384]{3,1,2,0:T(8,128)(2,1)} %constant_dynamic-update-slice_fusion), calls=%async_computation | async-start | bytes 786432 | tf_op jit(solution)/shard_map/all_to_all | solution.py:16
  29.6 0.1 multiply_select_fusion
  29.7 0.1 multiply_select_fusion.1
  29.9 0.3 multiply_bitcast_fusion
  30.2 2.3 %reshape.536 = f32[384,384,1]{1,0,2:T(8,128)} reshape(f32[16,24,16,24]{3,2,1,0:T(8,128)S(1)} %multiply_bitcast_fusion) | data formatting | bytes 1179648 | tf_op jit(solution)/shard_map/reshape | solution.py:54
  32.6 10.4 %all-to-all-done = bf16[32,12,1,384]{3,1,2,0:T(8,128)(2,1)S(1)} async-done(((bf16[32,12,1,384]{3,1,2,0:T(8,128)(2,1)}), bf16[32,12,1,384]{3,1,2,0:T(8,128)(2,1)S(1)}, u32[]{:S(2)}, u32[]{:S(2)}) %all-to-all-start) | async-done | bytes 294944 | tf_op jit(solution)/shard_map/all_to_all | solution.py:16
  43.0 1.8 %convolution_bitcast_fusion.1 = f32[32,12,384]{2,0,1:T(8,128)S(1)} fusion(f32[384,384,1]{1,0,2:T(8,128)} %reshape.536, bf16[12,32,1,384]{3,0,2,1:T(8,128)(2,1)S(1)} %bitcast.94), kind=kOutput, calls=%fused_computation.4 | convolution fusion | flops 679477248 | bytes 1474560 | tf_op jit(solution)/shard_map/zpc,cv->zpv/dot_general | solution.py:67
  44.8 0.4 copy.1188
  45.2 0.1 reshape.531
  45.2 0.9 convolution_bitcast_fusion
  46.2 0.1 fusion.55
  46.3 0.1 copy.1191
  46.4 1.5 %collective-permute-start.1 = (f32[1,24,384]{2,1,0:T(8,128)S(1)}, f32[1,24,384]{2,1,0:T(8,128)S(1)}, u32[]{:S(2)}, u32[]{:S(2)}) collective-permute-start(f32[1,24,384]{2,1,0:T(8,128)S(1)} %copy.1191), channel_id=1, source_target_pairs={{0,8},{8,16},{16,24},{1,9},{9,17},{17,25},{2,10},{10,18},{18,26},{... | collective-permute-start | bytes 110600 | tf_op jit(solution)/shard_map/ppermute | solution.py:32
  47.9 0.3 copy.1189
  48.2 0.3 reshape.532
  48.6 0.1 copy.1190
  48.6 1.3 %collective-permute-start = (f32[1,24,384]{2,1,0:T(8,128)S(1)}, f32[1,24,384]{2,1,0:T(8,128)S(1)}, u32[]{:S(2)}, u32[]{:S(2)}) collective-permute-start(f32[1,24,384]{2,1,0:T(8,128)S(1)} %copy.1190), channel_id=1, source_target_pairs={{8,0},{16,8},{24,16},{9,1},{17,9},{25,17},{10,2},{18,10},{26,18},{... | collective-permute-start | bytes 110600 | tf_op jit(solution)/shard_map/ppermute | solution.py:34
  50.0 4.9 %collective-permute-done = f32[1,24,384]{2,1,0:T(8,128)S(1)} collective-permute-done((f32[1,24,384]{2,1,0:T(8,128)S(1)}, f32[1,24,384]{2,1,0:T(8,128)S(1)}, u32[]{:S(2)}, u32[]{:S(2)}) %collective-permute-start) | collective-permute-done | bytes 36896 | tf_op jit(solution)/shard_map/ppermute | solution.py:34
  55.0 1.3 %collective-permute-start.2 = (f32[18,1,384]{2,1,0:T(1,128)S(1)}, f32[18,1,384]{2,1,0:T(1,128)S(1)}, u32[]{:S(2)}, u32[]{:S(2)}) collective-permute-start(f32[18,1,384]{2,1,0:T(1,128)S(1)} %get-tuple-element.9), channel_id=1, source_target_pairs={{1,0},{2,1},{3,2},{4,3},{5,4},{6,5},{7,6},{9,8},{10,9},{11,10},{12... | collective-permute-start | bytes 82952 | tf_op jit(solution)/shard_map/ppermute | solution.py:34
  56.3 3.0 %collective-permute-start.3 = (f32[18,1,384]{2,1,0:T(1,128)S(1)}, f32[18,1,384]{2,1,0:T(1,128)S(1)}, u32[]{:S(2)}, u32[]{:S(2)}) collective-permute-start(f32[18,1,384]{2,1,0:T(1,128)S(1)} %get-tuple-element.8), channel_id=1, source_target_pairs={{0,1},{1,2},{2,3},{3,4},{4,5},{5,6},{6,7},{8,9},{9,10},{10,11},{11... | collective-permute-start | bytes 82952 | tf_op jit(solution)/shard_map/ppermute | solution.py:32
  59.4 0.8 collective-permute-done.3
  60.2 0.6 select_maximum_fusion
  60.8 1.9 %multiply_reduce_fusion = (f32[]{:T(128)}, f32[16,24,384]{2,1,0:T(8,128)}) fusion(f32[16,24,384]{2,1,0:T(8,128)S(1)} %copy-done.1, f32[18,26,386]{2,1,0:T(8,128)S(1)} %select_maximum_fusion, f32[18,24,384]{2,1,0:T(8,128)S(1)} %constant_dynamic-update-slice_fusion.32, f32[18,1,384]{2,1,0:T(1,128)S(1)} %collective-permute-done.3, ...), kind=kLoop, calls=%fused_computation.21 | loop fusion | flops 2064383 | bytes 3741700 | tf_op jit(solution)/shard_map/reduce_sum | solution.py:101
  62.7 41.2 %psum.7 = f32[]{:T(128)} all-reduce(f32[]{:T(128)} %get-tuple-element.6), channel_id=1, replica_groups=mesh['px'=4,'py'=8] {'px','py'}, use_global_device_ids=true, to_apply=%region_1.2 | all-reduce | flops 1 | bytes 8 | tf_op jit(solution)/shard_map/psum | solution.py:102
  (20 shorter events, 0.2 us)
Async XLA Ops:
  0.7 1.2 %copy-start.2 = (s32[3,768]{1,0:T(4,128)S(1)}, s32[3,768]{1,0:T(4,128)}, u32[]{:S(2)}) copy-start(s32[3,768]{1,0:T(4,128)} %param.4) | copy-start | bytes 27652
  22.2 20.8 %all-to-all-start = ((bf16[32,12,1,384]{3,1,2,0:T(8,128)(2,1)}), bf16[32,12,1,384]{3,1,2,0:T(8,128)(2,1)S(1)}, u32[]{:S(2)}, u32[]{:S(2)}) async-start(bf16[32,12,1,384]{3,1,2,0:T(8,128)(2,1)} %constant_dynamic-update-slice_fusion), calls=%async_computation | async-start | bytes 786432 | tf_op jit(solution)/shard_map/all_to_all | solution.py:16
  46.4 3.6 %collective-permute-start.1 = (f32[1,24,384]{2,1,0:T(8,128)S(1)}, f32[1,24,384]{2,1,0:T(8,128)S(1)}, u32[]{:S(2)}, u32[]{:S(2)}) collective-permute-start(f32[1,24,384]{2,1,0:T(8,128)S(1)} %copy.1191), channel_id=1, source_target_pairs={{0,8},{8,16},{16,24},{1,9},{9,17},{17,25},{2,10},{10,18},{18,26},{... | collective-permute-start | bytes 110600 | tf_op jit(solution)/shard_map/ppermute | solution.py:32
  48.5 12.3 %copy-start = (f32[16,24,384]{2,1,0:T(8,128)}, f32[16,24,384]{2,1,0:T(8,128)S(1)}, u32[]{:S(2)}) copy-start(f32[16,24,384]{2,1,0:T(8,128)S(1)} %reshape.532) | copy-start | bytes 1769476
  48.6 6.3 %collective-permute-start = (f32[1,24,384]{2,1,0:T(8,128)S(1)}, f32[1,24,384]{2,1,0:T(8,128)S(1)}, u32[]{:S(2)}, u32[]{:S(2)}) collective-permute-start(f32[1,24,384]{2,1,0:T(8,128)S(1)} %copy.1190), channel_id=1, source_target_pairs={{8,0},{16,8},{24,16},{9,1},{17,9},{25,17},{10,2},{18,10},{26,18},{... | collective-permute-start | bytes 110600 | tf_op jit(solution)/shard_map/ppermute | solution.py:34
  50.0 10.8 %copy-start.1 = (f32[16,24,384]{2,1,0:T(8,128)S(1)}, f32[16,24,384]{2,1,0:T(8,128)}, u32[]{:S(2)}) copy-start(f32[16,24,384]{2,1,0:T(8,128)} %param.5) | copy-start | bytes 1769476
  55.0 4.3 %collective-permute-start.2 = (f32[18,1,384]{2,1,0:T(1,128)S(1)}, f32[18,1,384]{2,1,0:T(1,128)S(1)}, u32[]{:S(2)}, u32[]{:S(2)}) collective-permute-start(f32[18,1,384]{2,1,0:T(1,128)S(1)} %get-tuple-element.9), channel_id=1, source_target_pairs={{1,0},{2,1},{3,2},{4,3},{5,4},{6,5},{7,6},{9,8},{10,9},{11,10},{12... | collective-permute-start | bytes 82952 | tf_op jit(solution)/shard_map/ppermute | solution.py:34
  56.3 3.9 %collective-permute-start.3 = (f32[18,1,384]{2,1,0:T(1,128)S(1)}, f32[18,1,384]{2,1,0:T(1,128)S(1)}, u32[]{:S(2)}, u32[]{:S(2)}) collective-permute-start(f32[18,1,384]{2,1,0:T(1,128)S(1)} %get-tuple-element.8), channel_id=1, source_target_pairs={{0,1},{1,2},{2,3},{3,4},{4,5},{5,6},{6,7},{8,9},{9,10},{10,11},{11... | collective-permute-start | bytes 82952 | tf_op jit(solution)/shard_map/ppermute | solution.py:32
